TPU v7x, 32 devices: a whole 2x2x4 slice. The times are simulated.
32 devices in a mesh: dp: 4 (over y, x), shard: 8 (over z, core).
Axes of the slice: x: 2, y: 2, z: 4, core: 2. Of those that a mesh axis runs over, the one named last changes fastest.
Arguments:
- gradients: bfloat16 [4, 4, 786432], P('dp', None, 'shard'), may hold values from -32 to 32
- master: float32 [3145728], P(('dp', 'shard'))
- moment: float32 [3145728], P(('dp', 'shard')), may hold values from -1.5 to 1.5
- second: float32 [3145728], P(('dp', 'shard')), may hold values from 0.05 to 2
- segment_ids: int32 [24576], P(('dp', 'shard')), may hold values from 0 to 15, never falling along the last dimension, each value on 1 to 3072 neighbouring positions
Outputs:
- weights: bfloat16 [4, 786432], P(None, 'shard')
- new_master: float32 [3145728], P(('dp', 'shard'))
- new_moment: float32 [3145728], P(('dp', 'shard'))
- new_second: float32 [3145728], P(('dp', 'shard'))
Inputs may be any that keep to these rules, and one draw needn't show every extreme that they name: segment_ids never falls along the flat vector; each tensor has 1 to 3072 blocks and one has exactly 3072.
All inputs are finite; a program needn't handle non-finite values.
Results may differ from a plain program's by a relative error of at most 0.0004.
Values may be sent and summed in bfloat16 or wider, within the bound.
No kernel may reach another device: no remote copies, remote signals or barrier semaphores. Data moves between devices by JAX's collectives and lax.ppermute only.
A program may use at most 64 MiB of HBM per device.

v0:
```python
import jax
import jax.numpy as jnp
from jax import lax
from jax.sharding import PartitionSpec as P

first_fix = 1.0 - 0.9**20
second_fix = 1.0 - 0.999**20
learn_rate = 0.2
decay_rate = 0.01
tiny_eps = 1e-06


def moments(summed, master_part, moment_part, second_part, replicas):
    grad = summed / replicas
    next_moment = 0.9 * moment_part + 0.1 * grad
    next_second = 0.999 * second_part + 0.001 * grad * grad
    update_dir = (
        next_moment / first_fix / (jnp.sqrt(next_second / second_fix) + tiny_eps)
        + decay_rate * master_part
    )
    return (next_moment, next_second, update_dir)


def tensor_sums(values, onehot):
    block_sq = jnp.sum((values * values).reshape(onehot.shape[0], -1), axis=1)
    return jnp.dot(block_sq, onehot, precision=lax.Precision.HIGHEST)


def on_device(gradients, master, moment, second, segment_ids):
    replicas = lax.axis_size("dp")
    tensors = lax.axis_size("dp") * lax.axis_size("shard") // 2
    blocks = segment_ids.shape[0]
    onehot = (segment_ids[:, None] == jnp.arange(tensors, dtype=jnp.int32)[None, :]).astype(
        jnp.float32
    )
    received = lax.all_to_all(gradients[0], "dp", split_axis=0, concat_axis=0, tiled=True)
    summed = jnp.sum(received.astype(jnp.float32), axis=0)
    new_moment, new_second, update_dir = moments(summed, master, moment, second, replicas)
    weight_sq, update_sq = lax.psum(
        (tensor_sums(master, onehot), tensor_sums(update_dir, onehot)), ("dp", "shard")
    )
    trust = jnp.sqrt(weight_sq) / (jnp.sqrt(update_sq) + tiny_eps)
    block_trust = jnp.dot(onehot, trust, precision=lax.Precision.HIGHEST)
    new_master = master - learn_rate * (
        update_dir.reshape(blocks, -1) * block_trust[:, None]
    ).reshape(-1)
    rounded = new_master.astype(jnp.bfloat16)[None, :]
    weights = lax.all_gather(rounded, "dp", axis=0, tiled=True)
    return (weights, new_master, new_moment, new_second)


def solution(mesh):
    placed = (
        P("dp", None, "shard"),
        P(("dp", "shard")),
        P(("dp", "shard")),
        P(("dp", "shard")),
        P(("dp", "shard")),
    )
    return jax.shard_map(
        on_device,
        mesh=mesh,
        in_specs=placed,
        out_specs=(P(None, "shard"), P(("dp", "shard")), P(("dp", "shard")), P(("dp", "shard"))),
        check_vma=False,
    )
```

profile of v0, /device:TPU:0, one launch (start us, length us, event | category | flops | bytes accessed | tf_op | source)
XLA Modules:
  0.0 80.3 jit_solution(6110811445067844543)
XLA Ops:
  0.6 0.5 broadcast.17
  1.1 2.8 %reduce.3 = bf16[4,98304]{1,0:T(4,128)(2,1)S(1)} reduce(bf16[4,1,98304]{2,0,1:T(4,128)(2,1)} %bitcast.21, bf16[]{:T(256)} %broadcast.17), dimensions={1}, to_apply=%copy.10.reduce_sub_computation | reduce | bytes 1572866 | tf_op jit(solution)/shard_map/all_to_all | solution.py:36
  3.9 0.8 reshape.33
  4.7 16.3 %all_to_all.9 = bf16[4,2,49152]{2,1,0:T(2,128)(2,1)S(1)} all-to-all(bf16[4,2,49152]{2,1,0:T(2,128)(2,1)S(1)} %reshape.33), channel_id=1, replica_groups=mesh['dp'=4,'shard'=8] {'dp'}, dimensions={0} | all-to-all | bytes 1572864 | tf_op jit(solution)/shard_map/all_to_all | solution.py:36
  21.0 0.0 copy-start
  21.0 0.7 reshape.34
  21.8 2.4 %convert_reduce_fusion = f32[98304]{0:T(1024)S(1)} fusion(bf16[4,1,98304]{2,1,0:T(2,128)(2,1)S(1)} %reshape.34), kind=kLoop, calls=%fused_computation | loop fusion | flops 688128 | bytes 1179648 | tf_op jit(solution)/shard_map/reduce_sum | solution.py:37
  24.2 0.0 copy-done
  24.2 0.0 copy-done.3
  24.2 0.0 copy-done.4
  24.2 0.0 copy-start.5
  24.3 0.4 bitcast_reduce_fusion.1
  24.7 0.0 copy-start.1
  24.7 0.0 copy-start.2
  24.7 0.2 copy-done.5
  24.9 0.3 convolution_bitcast_fusion.1
  25.3 0.3 convolution_bitcast_fusion
  25.6 39.5 %all-reduce = (f32[16]{0:T(128)S(1)}, f32[16]{0:T(128)S(1)}) all-reduce(f32[16]{0:T(128)S(1)} %convolution_bitcast_fusion, f32[16]{0:T(128)S(1)} %convolution_bitcast_fusion.1), channel_id=1, replica_groups=mesh['dp'=4,'shard'=8] {'dp','shard'}, use_global_device_ids=true, to_apply=%region_4.0 | all-reduce | flops 32 | bytes 256 | tf_op jit(solution)/shard_map/psum | solution.py:39
  65.1 0.4 convolution_reduce_fusion
  65.5 1.0 %fusion.10 = (bf16[98304]{0:T(1024)(128)(2,1)S(1)}, f32[98304]{0:T(1024)}) fusion(f32[98304]{0:T(1024)S(1)} %copy-done, f32[768]{0:T(1024)S(1)} %convolution_reduce_fusion, f32[98304]{0:T(1024)S(1)} %get-tuple-element.11, f32[98304]{0:T(1024)S(1)} %get-tuple-element.10), kind=kLoop, calls=%fused_computation.22 | loop fusion | flops 983040 | bytes 1772544 | tf_op jit(solution)/shard_map/convert_element_type | solution.py:47
  66.5 12.6 %all-gather = bf16[393216]{0:T(1024)(128)(2,1)S(1)} all-gather(bf16[98304]{0:T(1024)(128)(2,1)S(1)} %get-tuple-element.8), channel_id=2, replica_groups=mesh['dp'=4,'shard'=8] {'dp'}, dimensions={0}, use_global_device_ids=true | all-gather | bytes 983040 | tf_op jit(solution)/shard_map/all_gather | solution.py:48
  79.1 1.2 %reshape.25 = bf16[4,98304]{1,0:T(4,128)(2,1)} reshape(bf16[393216]{0:T(1024)(128)(2,1)S(1)} %all-gather) | data formatting | bytes 1572864 | tf_op jit(solution)/shard_map/all_gather | solution.py:48
  80.3 0.0 copy-done.1
  80.3 0.0 copy-done.2
  (4 shorter events, 0.0 us)
Async XLA Ops:
  21.0 3.2 %copy-start = (f32[98304]{0:T(1024)S(1)}, f32[98304]{0:T(1024)}, u32[]{:S(2)}) copy-start(f32[98304]{0:T(1024)} %param.6) | copy-start | bytes 1179652
  21.0 3.2 %copy-start.3 = (f32[98304]{0:T(1024)S(1)}, f32[98304]{0:T(1024)}, u32[]{:S(2)}) copy-start(f32[98304]{0:T(1024)} %param.7) | copy-start | bytes 1179652
  21.0 3.2 %copy-start.4 = (f32[98304]{0:T(1024)S(1)}, f32[98304]{0:T(1024)}, u32[]{:S(2)}) copy-start(f32[98304]{0:T(1024)} %param.8) | copy-start | bytes 1179652
  24.2 0.7 copy-start.5
  24.7 55.6 %copy-start.1 = (f32[98304]{0:T(1024)}, f32[98304]{0:T(1024)S(1)}, u32[]{:S(2)}) copy-start(f32[98304]{0:T(1024)S(1)} %get-tuple-element.10) | copy-start | bytes 1179652
  24.7 55.6 %copy-start.2 = (f32[98304]{0:T(1024)}, f32[98304]{0:T(1024)S(1)}, u32[]{:S(2)}) copy-start(f32[98304]{0:T(1024)S(1)} %get-tuple-element.11) | copy-start | bytes 1179652
where the time goes:
time: 80.6 us; the launch traced here: 80.3 us
  blocking collectives  68.4 us (85%)
  other arithmetic  6.61 us (8%)
  local copies, waits for them, and re-layouts  3.45 us (4%)
  matrix products  1.05 us (1%)
    psum x1, blocking collectives, on_device(): lax.psum((tensor_sums(master, onehot), tensor_sums(update_dir, onehot)),...  39.5 us
    all_to_all x1, blocking collectives, on_device(): lax.all_to_all(gradients[0], 'dp', split_axis=0, concat_axis=0, tiled=True)  16.3 us
    all_gather x1, blocking collectives, on_device(): weights = lax.all_gather(rounded, 'dp', axis=0, tiled=True)  12.6 us
    all_to_all x1, other arithmetic, on_device(): lax.all_to_all(gradients[0], 'dp', split_axis=0, concat_axis=0, tiled=True)  2.75 us
    reduce_sum x1, other arithmetic, on_device(): summed = jnp.sum(received.astype(jnp.float32), axis=0)  2.43 us
    unnamed x14, local copies, waits for them, and re-layouts  1.76 us

commit v1 on v0

--- a/solution.py
+++ b/solution.py
@@ -36,8 +36,11 @@
     received = lax.all_to_all(gradients[0], "dp", split_axis=0, concat_axis=0, tiled=True)
     summed = jnp.sum(received.astype(jnp.float32), axis=0)
     new_moment, new_second, update_dir = moments(summed, master, moment, second, replicas)
-    weight_sq, update_sq = lax.psum(
-        (tensor_sums(master, onehot), tensor_sums(update_dir, onehot)), ("dp", "shard")
+    recast_kinds_on = lambda x_part, device_axis, across: jax.lax.psum(
+        jax.lax.psum(x_part, device_axis), axis_name=across
+    )
+    weight_sq, update_sq = recast_kinds_on(
+        (tensor_sums(master, onehot), tensor_sums(update_dir, onehot)), "shard", "dp"
     )
     trust = jnp.sqrt(weight_sq) / (jnp.sqrt(update_sq) + tiny_eps)
     block_trust = jnp.dot(onehot, trust, precision=lax.Precision.HIGHEST)

time: 80.6 us -> 63.4 us (0.79)
  blocking collectives: 68.4 us -> 51.2 us
    psum x1 -> x2, blocking collectives: 39.5 us -> 23.9 us  [the longest x1 15.1 us: on_device(): jax.lax.psum(x_part, device_axis)]
    all_gather x1, blocking collectives: 12.6 us -> 11 us  [on_device(): weights = lax.all_gather(rounded, 'dp', axis=0, tiled=True)]
where the time goes in v1:
time: 63.4 us; the launch traced here: 63.1 us
  blocking collectives  51.2 us (81%)
  other arithmetic  6.61 us (10%)
  local copies, waits for them, and re-layouts  3.45 us (5%)
  matrix products  1.06 us (2%)
  between operations  0.75 us (1%)
    all_to_all x1, blocking collectives, on_device(): lax.all_to_all(gradients[0], 'dp', split_axis=0, concat_axis=0, tiled=True)  16.3 us
    psum x1, blocking collectives, on_device(): jax.lax.psum(x_part, device_axis)  15.1 us
    all_gather x1, blocking collectives, on_device(): weights = lax.all_gather(rounded, 'dp', axis=0, tiled=True)  11 us
    psum x1, blocking collectives, on_device(): jax.lax.psum(jax.lax.psum(x_part, device_axis), axis_name=across)  8.72 us
    all_to_all x1, other arithmetic, on_device(): lax.all_to_all(gradients[0], 'dp', split_axis=0, concat_axis=0, tiled=True)  2.75 us
    reduce_sum x1, other arithmetic, on_device(): summed = jnp.sum(received.astype(jnp.float32), axis=0)  2.43 us
    unnamed x14, local copies, waits for them, and re-layouts  1.76 us

profile of v1, /device:TPU:0, one launch (start us, length us, event | category | flops | bytes accessed | tf_op | source)
XLA Modules:
  0.0 63.1 jit_solution(11203071899683855664)
XLA Ops:
  0.6 0.5 broadcast.17
  1.1 2.8 %reduce.3 = bf16[4,98304]{1,0:T(4,128)(2,1)S(1)} reduce(bf16[4,1,98304]{2,0,1:T(4,128)(2,1)} %bitcast.21, bf16[]{:T(256)} %broadcast.17), dimensions={1}, to_apply=%copy.10.reduce_sub_computation | reduce | bytes 1572866 | tf_op jit(solution)/shard_map/all_to_all | solution.py:36
  3.9 0.8 %reshape.33 = bf16[4,2,49152]{2,1,0:T(2,128)(2,1)S(1)} reshape(bf16[4,98304]{1,0:T(4,128)(2,1)S(1)} %reduce.3) | data formatting | bytes 1572864
  4.7 16.3 %all_to_all.9 = bf16[4,2,49152]{2,1,0:T(2,128)(2,1)S(1)} all-to-all(bf16[4,2,49152]{2,1,0:T(2,128)(2,1)S(1)} %reshape.33), channel_id=1, replica_groups=mesh['dp'=4,'shard'=8] {'dp'}, dimensions={0} | all-to-all | bytes 1572864 | tf_op jit(solution)/shard_map/all_to_all | solution.py:36
  21.0 0.7 %reshape.34 = bf16[4,1,98304]{2,1,0:T(2,128)(2,1)S(1)} reshape(bf16[4,2,49152]{2,1,0:T(2,128)(2,1)S(1)} %all_to_all.9) | data formatting | bytes 1572864
  21.8 2.4 %convert_reduce_fusion = f32[98304]{0:T(1024)S(1)} fusion(bf16[4,1,98304]{2,1,0:T(2,128)(2,1)S(1)} %reshape.34), kind=kLoop, calls=%fused_computation | loop fusion | flops 688128 | bytes 1179648 | tf_op jit(solution)/shard_map/reduce_sum | solution.py:37
  24.2 0.0 copy-done
  24.2 0.0 copy-done.3
  24.2 0.0 copy-done.4
  24.2 0.0 copy-start.5
  24.3 0.4 bitcast_reduce_fusion.1
  24.7 0.0 copy-start.1
  24.7 0.0 copy-start.2
  24.7 0.2 copy-done.5
  24.9 0.3 convolution_bitcast_fusion.1
  25.3 0.3 convolution_bitcast_fusion
  25.6 15.1 %all-reduce = (f32[16]{0:T(128)S(1)}, f32[16]{0:T(128)S(1)}) all-reduce(f32[16]{0:T(128)S(1)} %convolution_bitcast_fusion, f32[16]{0:T(128)S(1)} %convolution_bitcast_fusion.1), channel_id=1, replica_groups=mesh['dp'=4,'shard'=8] {'shard'}, use_global_device_ids=true, to_apply=%region_5.0 | all-reduce | flops 32 | bytes 256 | tf_op jit(solution)/shard_map/psum | solution.py:40
  40.7 8.7 %all-reduce.1 = (f32[16]{0:T(128)S(1)}, f32[16]{0:T(128)S(1)}) all-reduce(f32[16]{0:T(128)S(1)} %get-tuple-element.6, f32[16]{0:T(128)S(1)} %get-tuple-element.7), channel_id=1, replica_groups=mesh['dp'=4,'shard'=8] {'dp'}, use_global_device_ids=true, to_apply=%region_6.0 | all-reduce | flops 32 | bytes 256 | tf_op jit(solution)/shard_map/psum | solution.py:39
  49.5 0.4 convolution_reduce_fusion
  49.9 1.0 %fusion.10 = (bf16[98304]{0:T(1024)(128)(2,1)S(1)}, f32[98304]{0:T(1024)}) fusion(f32[98304]{0:T(1024)S(1)} %copy-done, f32[768]{0:T(1024)S(1)} %convolution_reduce_fusion, f32[98304]{0:T(1024)S(1)} %get-tuple-element.13, f32[98304]{0:T(1024)S(1)} %get-tuple-element.12), kind=kLoop, calls=%fused_computation.22 | loop fusion | flops 983040 | bytes 1772544 | tf_op jit(solution)/shard_map/convert_element_type | solution.py:50
  50.9 11.0 %all-gather = bf16[393216]{0:T(1024)(128)(2,1)S(1)} all-gather(bf16[98304]{0:T(1024)(128)(2,1)S(1)} %get-tuple-element.10), channel_id=2, replica_groups=mesh['dp'=4,'shard'=8] {'dp'}, dimensions={0}, use_global_device_ids=true | all-gather | bytes 983040 | tf_op jit(solution)/shard_map/all_gather | solution.py:51
  61.9 0.0 copy-done.1
  61.9 0.0 copy-done.2
  61.9 1.2 %reshape.25 = bf16[4,98304]{1,0:T(4,128)(2,1)} reshape(bf16[393216]{0:T(1024)(128)(2,1)S(1)} %all-gather) | data formatting | bytes 1572864 | tf_op jit(solution)/shard_map/all_gather | solution.py:51
  (5 shorter events, 0.0 us)
Async XLA Ops:
  21.0 3.2 %copy-start = (f32[98304]{0:T(1024)S(1)}, f32[98304]{0:T(1024)}, u32[]{:S(2)}) copy-start(f32[98304]{0:T(1024)} %param.6) | copy-start | bytes 1179652
  21.0 3.2 %copy-start.3 = (f32[98304]{0:T(1024)S(1)}, f32[98304]{0:T(1024)}, u32[]{:S(2)}) copy-start(f32[98304]{0:T(1024)} %param.7) | copy-start | bytes 1179652
  21.0 3.2 %copy-start.4 = (f32[98304]{0:T(1024)S(1)}, f32[98304]{0:T(1024)}, u32[]{:S(2)}) copy-start(f32[98304]{0:T(1024)} %param.8) | copy-start | bytes 1179652
  24.2 0.7 %copy-start.5 = (s32[768]{0:T(1024)S(1)}, s32[768]{0:T(1024)}, u32[]{:S(2)}) copy-start(s32[768]{0:T(1024)} %param.9) | copy-start | bytes 9220
  24.7 37.2 %copy-start.1 = (f32[98304]{0:T(1024)}, f32[98304]{0:T(1024)S(1)}, u32[]{:S(2)}) copy-start(f32[98304]{0:T(1024)S(1)} %get-tuple-element.12) | copy-start | bytes 1179652
  24.7 37.2 %copy-start.2 = (f32[98304]{0:T(1024)}, f32[98304]{0:T(1024)S(1)}, u32[]{:S(2)}) copy-start(f32[98304]{0:T(1024)S(1)} %get-tuple-element.13) | copy-start | bytes 1179652
